TPU v7x, 32 devices: a whole 2x2x4 slice. The times are simulated.
32 devices in a mesh: gy: 2 (over core), gx: 16 (over z, y, x).
Axes of the slice: x: 2, y: 2, z: 4, core: 2. Of those that a mesh axis runs over, the one named last changes fastest.
Arguments:
- basis_vectors: float32 [36, 64, 128, 256], P(None, 'gx', 'gy'), may hold values from -30 to 30, as said below
- reaction: float32 [64, 128, 256], P('gx', 'gy'), may hold values from 0.5 to 3
Outputs:
- new_vectors: float32 [4, 64, 128, 256], P(None, 'gx', 'gy')
- hessenberg: float32 [40, 4], replicated
Inputs may be any that keep to these rules, and one draw needn't show every extreme that they name: `basis_vectors`: under the inner product the basis vectors are nearly orthonormal.
All inputs are finite; a program needn't handle non-finite values.
Results may differ from a plain program's by a relative error of at most 0.0003.
Values sent between devices are 32-bit elements; how exact they have to be, the bound alone decides.
A program may use at most 128 MiB of HBM per device.

v0:
```python
import jax
import jax.numpy as jnp
from jax import lax
from jax.sharding import PartitionSpec as P

STEPS = 4
WIND_SPEEDS = (0.9, 0.6, 0.4)
EPSILON = 1e-06


def with_halo(cells, sides, width):
    for axis, dim in sides:
        count = lax.axis_size(axis)
        ends = count - 1
        head = lax.slice_in_dim(cells, 0, width, axis=dim)
        tail = lax.slice_in_dim(cells, cells.shape[dim] - width, cells.shape[dim], axis=dim)
        cells = jnp.concatenate(
            [
                lax.ppermute(tail, axis, [(i, (i + 1) % count) for i in range(ends)]),
                cells,
                lax.ppermute(head, axis, [((i + 1) % count, i) for i in range(ends)]),
            ],
            axis=dim,
        )
    return cells


def stencil(values, x_ext, y_ext, z_ext, reaction):
    summed = -reaction * values
    for position, extended in enumerate((x_ext, y_ext, z_ext)):
        count = values.shape[position]
        higher = lax.slice_in_dim(extended, 3, count + 3, axis=position)
        lower_one = lax.slice_in_dim(extended, 1, count + 1, axis=position)
        lower_two = lax.slice_in_dim(extended, 0, count, axis=position)
        wind_speed = WIND_SPEEDS[position]
        summed = (
            summed
            + higher
            + lower_one
            - 2.0 * values
            - wind_speed * (3.0 * values - 4.0 * lower_one + lower_two) * 0.5
        )
    return summed


def apply_operator(values, reaction):
    rows_x = values.shape[0]
    rows_y = values.shape[1]
    padded = with_halo(values, (("gy", 1), ("gx", 0)), 2)
    x_ext = padded[: rows_x + 3, 2 : rows_y + 2]
    y_ext = padded[2 : rows_x + 2, : rows_y + 3]
    z_ext = jnp.pad(values, ((0, 0), (0, 0), (2, 1)))
    return stencil(values, x_ext, y_ext, z_ext, reaction)


def project(basis_vectors, created, image):
    local = jnp.einsum("kxyz,xyz->k", basis_vectors, image, precision=lax.Precision.HIGHEST)
    extra = [jnp.sum(vector * image)[None] for vector in created]
    return jnp.concatenate([local] + extra)


def combine(basis_vectors, created, weights):
    keep_count = basis_vectors.shape[0]
    summed = jnp.einsum(
        "k,kxyz->xyz", weights[:keep_count], basis_vectors, precision=lax.Precision.HIGHEST
    )
    for index, vector in enumerate(created):
        summed = summed + weights[keep_count + index] * vector
    return summed


def body(basis_vectors, reaction):
    keep_count = basis_vectors.shape[0]
    basis_size = keep_count + STEPS
    cell_count = float(
        basis_vectors.shape[1]
        * basis_vectors.shape[2]
        * basis_vectors.shape[3]
        * lax.axis_size("gx")
        * lax.axis_size("gy")
    )
    created = []
    columns = []
    local_gram = jnp.einsum(
        "axyz,bxyz->ab", basis_vectors, basis_vectors, precision=lax.Precision.HIGHEST
    )
    kept_gram = lax.psum(local_gram, ("gy", "gx")) / cell_count
    gram_matrix = (
        jnp.zeros((basis_size, basis_size), jnp.float32).at[:keep_count, :keep_count].set(kept_gram)
    )
    for section in range(STEPS):
        current = keep_count + section
        vector_now = basis_vectors[keep_count - 1] if section == 0 else created[-1]
        image = apply_operator(vector_now, reaction)
        first_terms = lax.psum(project(basis_vectors, created, image), ("gy", "gx")) / cell_count
        first_rest = image - combine(basis_vectors, created, first_terms)
        second_terms, rest_square = lax.psum(
            (project(basis_vectors, created, first_rest), jnp.sum(first_rest * first_rest)),
            ("gy", "gx"),
        )
        second_terms = second_terms / cell_count
        rest_square = rest_square / cell_count
        gram_now = gram_matrix[:current, :current]
        folded = jnp.dot(gram_now, second_terms, precision=lax.Precision.HIGHEST)
        second_rest = first_rest - combine(basis_vectors, created, second_terms)
        squared = (
            rest_square
            - 2.0 * jnp.sum(second_terms * second_terms)
            + jnp.sum(second_terms * folded)
        )
        length_now = jnp.sqrt(squared + EPSILON)
        cross_terms = (second_terms - folded) / length_now
        gram_matrix = gram_matrix.at[:current, current].set(cross_terms)
        gram_matrix = gram_matrix.at[current, :current].set(cross_terms)
        gram_matrix = gram_matrix.at[current, current].set(squared / (length_now * length_now))
        weights = first_terms + second_terms
        columns.append(
            jnp.concatenate(
                [weights, length_now[None], jnp.zeros((basis_size - current - 1,), jnp.float32)]
            )
        )
        created.append(second_rest / length_now)
    return (jnp.stack(created), jnp.stack(columns, axis=1))


def solution(mesh):
    in_specs = (P(None, "gx", "gy", None), P("gx", "gy", None))
    out_specs = (P(None, "gx", "gy", None), P())
    return jax.shard_map(body, mesh=mesh, in_specs=in_specs, out_specs=out_specs, check_vma=False)
```

profile of v0, /device:TPU:0, one launch (start us, length us, event | category | flops | bytes accessed | tf_op | source)
XLA Modules:
  0.0 709.3 jit_solution(1123148927254146616)
XLA Ops:
  0.7 1.1 slice_bitcast_fusion
  1.8 1.6 collective-permute-start.1
  3.4 3.2 collective-permute-start
  6.6 25.4 %fusion.34 = f32[36,36]{1,0:T(8,128)S(1)} fusion(f32[36,4,64,256]{3,2,1,0:T(8,128)} %param.22), kind=kOutput, calls=%fused_computation.34 | convolution fusion | flops 1019215872 | bytes 9442368 | tf_op jit(solution)/shard_map/axyz,bxyz->ab/dot_general | solution.py:84
  34.7 4.7 collective-permute-start.3
  40.0 1.5 collective-permute-start.2
  42.1 5.0 collective-permute-done.2
  47.6 13.0 %fusion.38 = f32[36]{0:T(128)S(1)} fusion(f32[36,4,64,256]{3,2,1,0:T(8,128)S(1)} %copy-done, f32[4,64,256,1]{2,1,0,3:T(8,128)S(1)} %bitcast.235), kind=kOutput, calls=%fused_computation.40 | convolution fusion | flops 28311552 | bytes 9699472 | tf_op jit(solution)/shard_map/kxyz,xyz->k/dot_general | solution.py:57
  61.3 42.1 %psum.91 = f32[36]{0:T(128)S(1)} all-reduce(f32[36]{0:T(128)S(1)} %fusion.38), channel_id=1, replica_groups=mesh['gy'=2,'gx'=16] {'gy','gx'}, use_global_device_ids=true, to_apply=%region_0.0 | all-reduce | flops 36 | bytes 288 | tf_op jit(solution)/shard_map/psum | solution.py:95
  103.4 14.5 %fusion.26 = f32[1,4,64,256]{3,0,2,1:T(1,128)S(1)} fusion(f32[36,4,64,256]{3,2,1,0:T(8,128)} %param.22, f32[36]{0:T(128)S(1)} %psum.91), kind=kOutput, calls=%fused_computation.26 | convolution fusion | flops 28311588 | bytes 9699472 | tf_op jit(solution)/shard_map/k,kxyz->xyz/dot_general | solution.py:64
  118.6 15.8 %fusion.41 = f32[36]{0:T(128)S(1)} fusion(f32[36,4,64,256]{3,2,1,0:T(8,128)} %param.22, f32[4,64,256,1]{2,1,0,3:T(8,128)S(1)} %get-tuple-element.159), kind=kOutput, calls=%fused_computation.41 | convolution fusion | flops 28311552 | bytes 9699472 | tf_op jit(solution)/shard_map/kxyz,xyz->k/dot_general | solution.py:57
  134.4 39.9 %all-reduce.8 = (f32[36]{0:T(128)S(1)}, f32[]{:T(128)}, f32[36,36]{1,0:T(8,128)S(1)}) all-reduce(f32[36]{0:T(128)S(1)} %fusion.41, f32[]{:T(128)} %get-tuple-element.158, f32[36,36]{1,0:T(8,128)S(1)} %fusion.34), channel_id=1, replica_groups=mesh['gy'=2,'gx'=16] {'gy','gx'}, use_global_device_ids=true, to_apply=%region_1.0 | all-reduce | flops 1333 | bytes 10664 | tf_op jit(solution)/shard_map/psum | solution.py:97
  175.1 14.5 %fusion.22 = f32[1,4,64,256]{3,0,2,1:T(1,128)S(1)} fusion(f32[36,4,64,256]{3,2,1,0:T(8,128)} %param.22, f32[36]{0:T(128)S(1)} %get-tuple-element.148), kind=kOutput, calls=%fused_computation.22 | convolution fusion | flops 28311588 | bytes 9699472 | tf_op jit(solution)/shard_map/k,kxyz->xyz/dot_general | solution.py:64
  191.7 1.3 collective-permute-start.5
  193.0 3.0 collective-permute-start.4
  196.9 1.3 collective-permute-start.6
  198.2 4.8 collective-permute-start.7
  203.0 1.9 dynamic-slice_select_fusion.2
  205.0 1.7 scatter.35
  207.0 2.1 collective-permute-done.7
  210.2 16.0 %fusion.44 = f32[36]{0:T(128)S(1)} fusion(f32[36,4,64,256]{3,2,1,0:T(8,128)} %param.22, f32[4,64,256,1]{2,1,0,3:T(8,128)S(1)} %bitcast.241), kind=kOutput, calls=%fused_computation.42 | convolution fusion | flops 28311552 | bytes 9699472 | tf_op jit(solution)/shard_map/kxyz,xyz->k/dot_general | solution.py:57
  226.9 41.7 %psum.95 = f32[37]{0:T(128)S(1)} all-reduce(f32[37]{0:T(128)S(1)} %pad_maximum_fusion.26), channel_id=1, replica_groups=mesh['gy'=2,'gx'=16] {'gy','gx'}, use_global_device_ids=true, to_apply=%region_8.9 | all-reduce | flops 37 | bytes 296 | tf_op jit(solution)/shard_map/psum | solution.py:95
  269.2 14.5 %fusion.18 = f32[1,4,64,256]{3,0,2,1:T(1,128)S(1)} fusion(f32[36,4,64,256]{3,2,1,0:T(8,128)} %param.22, f32[37]{0:T(128)S(1)} %broadcast_multiply_fusion.6), kind=kOutput, calls=%fused_computation.18 | convolution fusion | flops 28311552 | bytes 9699476 | tf_op jit(solution)/shard_map/k,kxyz->xyz/dot_general | solution.py:64
  283.6 1.4 multiply_reduce_fusion.12
  285.1 16.1 %fusion.47 = f32[36]{0:T(128)S(1)} fusion(f32[36,4,64,256]{3,2,1,0:T(8,128)} %param.22, f32[4,64,256,1]{2,1,0,3:T(8,128)S(1)} %bitcast.236), kind=kOutput, calls=%fused_computation.43 | convolution fusion | flops 28311552 | bytes 9699472 | tf_op jit(solution)/shard_map/kxyz,xyz->k/dot_general | solution.py:57
  301.9 39.9 %all-reduce.7 = (f32[37]{0:T(128)S(1)}, f32[]{:T(128)}) all-reduce(f32[37]{0:T(128)S(1)} %pad_maximum_fusion.27, f32[]{:T(128)} %get-tuple-element.134), channel_id=1, replica_groups=mesh['gy'=2,'gx'=16] {'gy','gx'}, use_global_device_ids=true, to_apply=%region_10.11 | all-reduce | flops 38 | bytes 304 | tf_op jit(solution)/shard_map/psum | solution.py:97
  345.1 14.5 %fusion.14 = f32[1,4,64,256]{3,0,2,1:T(1,128)S(1)} fusion(f32[36,4,64,256]{3,2,1,0:T(8,128)} %param.22, f32[37]{0:T(128)S(1)} %get-tuple-element.197), kind=kOutput, calls=%fused_computation.14 | convolution fusion | flops 28311552 | bytes 9699476 | tf_op jit(solution)/shard_map/k,kxyz->xyz/dot_general | solution.py:64
  360.2 1.3 collective-permute-start.9
  361.5 3.0 collective-permute-start.8
  365.4 1.3 collective-permute-start.10
  366.7 4.8 collective-permute-start.11
  371.5 1.9 dynamic-slice_select_fusion.1
  373.5 1.7 scatter.40
  375.5 2.7 collective-permute-done.11
  378.3 1.1 multiply_reduce_fusion.11
  379.4 16.3 %fusion.50 = f32[36]{0:T(128)S(1)} fusion(f32[36,4,64,256]{3,2,1,0:T(8,128)} %param.22, f32[4,64,256,1]{2,1,0,3:T(8,128)S(1)} %bitcast.240), kind=kOutput, calls=%fused_computation.44 | convolution fusion | flops 28311552 | bytes 9699472 | tf_op jit(solution)/shard_map/kxyz,xyz->k/dot_general | solution.py:57
  395.8 1.4 pad_maximum_fusion.28
  397.1 41.7 %psum.98 = f32[38]{0:T(128)S(1)} all-reduce(f32[38]{0:T(128)S(1)} %pad_maximum_fusion.28), channel_id=1, replica_groups=mesh['gy'=2,'gx'=16] {'gy','gx'}, use_global_device_ids=true, to_apply=%region_18.19 | all-reduce | flops 38 | bytes 304 | tf_op jit(solution)/shard_map/psum | solution.py:95
  439.5 14.5 %fusion.10 = f32[1,4,64,256]{3,0,2,1:T(1,128)S(1)} fusion(f32[36,4,64,256]{3,2,1,0:T(8,128)} %param.22, f32[38]{0:T(128)S(1)} %broadcast_multiply_fusion.4), kind=kOutput, calls=%fused_computation.10 | convolution fusion | flops 28311552 | bytes 9699480 | tf_op jit(solution)/shard_map/k,kxyz->xyz/dot_general | solution.py:64
  454.0 2.0 multiply_reduce_fusion.7
  456.0 16.0 %fusion.53 = f32[36]{0:T(128)S(1)} fusion(f32[36,4,64,256]{3,2,1,0:T(8,128)} %param.22, f32[4,64,256,1]{2,1,0,3:T(8,128)S(1)} %bitcast.239), kind=kOutput, calls=%fused_computation.45 | convolution fusion | flops 28311552 | bytes 9699472 | tf_op jit(solution)/shard_map/kxyz,xyz->k/dot_general | solution.py:57
  472.0 1.3 pad_maximum_fusion.29
  473.3 39.1 %all-reduce.6 = (f32[38]{0:T(128)S(1)}, f32[]{:T(128)}) all-reduce(f32[38]{0:T(128)S(1)} %pad_maximum_fusion.29, f32[]{:T(128)} %get-tuple-element.129), channel_id=1, replica_groups=mesh['gy'=2,'gx'=16] {'gy','gx'}, use_global_device_ids=true, to_apply=%region_21.22 | all-reduce | flops 39 | bytes 312 | tf_op jit(solution)/shard_map/psum | solution.py:97
  515.9 14.5 %fusion.6 = f32[1,4,64,256]{3,0,2,1:T(1,128)S(1)} fusion(f32[36,4,64,256]{3,2,1,0:T(8,128)} %param.22, f32[38]{0:T(128)S(1)} %get-tuple-element.188), kind=kOutput, calls=%fused_computation.6 | convolution fusion | flops 28311552 | bytes 9699480 | tf_op jit(solution)/shard_map/k,kxyz->xyz/dot_general | solution.py:64
  530.3 1.3 fusion.141
  531.7 1.3 collective-permute-start.13
  533.0 3.0 collective-permute-start.12
  536.9 4.2 collective-permute-start.15
  541.1 2.0 dynamic-slice_select_fusion
  543.0 1.3 collective-permute-start.14
  544.4 1.6 scatter.45
  546.5 4.2 collective-permute-done.14
  550.7 1.1 multiply_reduce_fusion.6
  551.9 16.3 %fusion.56 = f32[36]{0:T(128)S(1)} fusion(f32[36,4,64,256]{3,2,1,0:T(8,128)} %param.22, f32[4,64,256,1]{2,1,0,3:T(8,128)S(1)} %bitcast.237), kind=kOutput, calls=%fused_computation.46 | convolution fusion | flops 28311552 | bytes 9699472 | tf_op jit(solution)/shard_map/kxyz,xyz->k/dot_general | solution.py:57
  568.1 2.1 pad_maximum_fusion.30
  570.2 41.5 %psum.101 = f32[39]{0:T(128)S(1)} all-reduce(f32[39]{0:T(128)S(1)} %pad_maximum_fusion.30), channel_id=1, replica_groups=mesh['gy'=2,'gx'=16] {'gy','gx'}, use_global_device_ids=true, to_apply=%region_30.31 | all-reduce | flops 39 | bytes 312 | tf_op jit(solution)/shard_map/psum | solution.py:95
  612.3 14.5 %fusion.2 = f32[1,4,64,256]{3,0,2,1:T(1,128)S(1)} fusion(f32[36,4,64,256]{3,2,1,0:T(8,128)} %param.22, f32[39]{0:T(128)S(1)} %broadcast_multiply_fusion.2), kind=kOutput, calls=%fused_computation.2 | convolution fusion | flops 28311552 | bytes 9699484 | tf_op jit(solution)/shard_map/k,kxyz->xyz/dot_general | solution.py:64
  626.8 2.8 multiply_reduce_fusion
  629.6 16.0 %fusion.59 = f32[36]{0:T(128)S(1)} fusion(f32[36,4,64,256]{3,2,1,0:T(8,128)} %param.22, f32[4,64,256,1]{2,1,0,3:T(8,128)S(1)} %bitcast.238), kind=kOutput, calls=%fused_computation.47 | convolution fusion | flops 28311552 | bytes 9699472 | tf_op jit(solution)/shard_map/kxyz,xyz->k/dot_general | solution.py:57
  645.7 2.0 pad_maximum_fusion.31
  647.6 39.2 %all-reduce.5 = (f32[39]{0:T(128)S(1)}, f32[]{:T(128)}) all-reduce(f32[39]{0:T(128)S(1)} %pad_maximum_fusion.31, f32[]{:T(128)} %get-tuple-element.122), channel_id=1, replica_groups=mesh['gy'=2,'gx'=16] {'gy','gx'}, use_global_device_ids=true, to_apply=%region_34.35 | all-reduce | flops 40 | bytes 320 | tf_op jit(solution)/shard_map/psum | solution.py:97
  688.1 14.5 %fusion.28 = f32[1,4,64,256]{3,0,2,1:T(1,128)S(1)} fusion(f32[36,4,64,256]{3,2,1,0:T(8,128)} %param.22, f32[39]{0:T(128)S(1)} %get-tuple-element.181), kind=kOutput, calls=%fused_computation.28 | convolution fusion | flops 28311552 | bytes 9699484 | tf_op jit(solution)/shard_map/k,kxyz->xyz/dot_general | solution.py:64
  706.0 2.0 fusion.135
  708.0 1.1 pad_maximum_fusion
  (89 shorter events, 21.0 us)
Async XLA Ops:
  0.6 31.3 %copy-start.2 = (s32[2]{0:T(128)S(1)}, s32[2]{0:T(128)}, u32[]{:S(2)}) copy-start(s32[2]{0:T(128)} %constant.309.clone.1) | copy-start | bytes 28
  0.6 32.0 %copy-start.4 = (s32[2]{0:T(128)S(1)}, s32[2]{0:T(128)}, u32[]{:S(2)}) copy-start(s32[2]{0:T(128)} %constant.307.clone.1) | copy-start | bytes 28
  0.7 32.7 %copy-start.3 = (s32[2]{0:T(128)S(1)}, s32[2]{0:T(128)}, u32[]{:S(2)}) copy-start(s32[2]{0:T(128)} %constant.304.clone.1) | copy-start | bytes 28
  0.7 46.9 %copy-start = (f32[36,4,64,256]{3,2,1,0:T(8,128)S(1)}, f32[36,4,64,256]{3,2,1,0:T(8,128)}, u32[]{:S(2)}) copy-start(f32[36,4,64,256]{3,2,1,0:T(8,128)} %param.22) | copy-start | bytes 28311556
  0.7 46.5 %copy-start.1 = (f32[4,64,256]{2,1,0:T(8,128)S(1)}, f32[4,64,256]{2,1,0:T(8,128)}, u32[]{:S(2)}) copy-start(f32[4,64,256]{2,1,0:T(8,128)} %param.23) | copy-start | bytes 786436
  1.8 32.7 %collective-permute-start.1 = (f32[4,2,256]{2,1,0:T(2,128)S(1)}, f32[4,2,256]{2,1,0:T(2,128)S(1)}, u32[]{:S(2)}, u32[]{:S(2)}) collective-permute-start(f32[4,2,256]{2,1,0:T(2,128)S(1)} %get-tuple-element.174), channel_id=1, source_target_pairs={{16,0},{17,1},{18,2},{19,3},{20,4},{21,5},{22,6},{23,7},{24,8},{25... | collective-permute-start | bytes 24584 | tf_op jit(solution)/shard_map/ppermute | solution.py:21
  3.4 31.2 %collective-permute-start = (f32[4,2,256]{2,1,0:T(2,128)S(1)}, f32[4,2,256]{2,1,0:T(2,128)S(1)}, u32[]{:S(2)}, u32[]{:S(2)}) collective-permute-start(f32[4,2,256]{2,1,0:T(2,128)S(1)} %get-tuple-element.175), channel_id=1, source_target_pairs={{0,16},{1,17},{2,18},{3,19},{4,20},{5,21},{6,22},{7,23},{8,24},{9,... | collective-permute-start | bytes 24584 | tf_op jit(solution)/shard_map/ppermute | solution.py:19
  34.7 7.4 %collective-permute-start.3 = (f32[2,68,256]{2,1,0:T(8,128)S(1)}, f32[2,68,256]{2,1,0:T(8,128)S(1)}, u32[]{:S(2)}, u32[]{:S(2)}) collective-permute-start(f32[2,68,256]{2,1,0:T(8,128)S(1)} %get-tuple-element.167), channel_id=1, source_target_pairs={{0,1},{1,2},{2,3},{3,4},{4,5},{5,6},{6,7},{7,8},{8,9},{9,10},{10,1... | collective-permute-start | bytes 417800 | tf_op jit(solution)/shard_map/ppermute | solution.py:19
  40.0 7.1 %collective-permute-start.2 = (f32[2,68,256]{2,1,0:T(8,128)S(1)}, f32[2,68,256]{2,1,0:T(8,128)S(1)}, u32[]{:S(2)}, u32[]{:S(2)}) collective-permute-start(f32[2,68,256]{2,1,0:T(8,128)S(1)} %get-tuple-element.166), channel_id=1, source_target_pairs={{1,0},{2,1},{3,2},{4,3},{5,4},{6,5},{7,6},{8,7},{9,8},{10,9},{11,1... | collective-permute-start | bytes 417800 | tf_op jit(solution)/shard_map/ppermute | solution.py:21
  191.7 4.5 collective-permute-start.5
  193.0 3.8 collective-permute-start.4
  196.9 12.3 %collective-permute-start.6 = (f32[2,68,256]{2,1,0:T(8,128)S(1)}, f32[2,68,256]{2,1,0:T(8,128)S(1)}, u32[]{:S(2)}, u32[]{:S(2)}) collective-permute-start(f32[2,68,256]{2,1,0:T(8,128)S(1)} %get-tuple-element.164), channel_id=1, source_target_pairs={{1,0},{2,1},{3,2},{4,3},{5,4},{6,5},{7,6},{8,7},{9,8},{10,9},{11,1... | collective-permute-start | bytes 417800 | tf_op jit(solution)/shard_map/ppermute | solution.py:21
  198.2 10.9 %collective-permute-start.7 = (f32[2,68,256]{2,1,0:T(8,128)S(1)}, f32[2,68,256]{2,1,0:T(8,128)S(1)}, u32[]{:S(2)}, u32[]{:S(2)}) collective-permute-start(f32[2,68,256]{2,1,0:T(8,128)S(1)} %get-tuple-element.165), channel_id=1, source_target_pairs={{0,1},{1,2},{2,3},{3,4},{4,5},{5,6},{6,7},{7,8},{8,9},{9,10},{10,1... | collective-permute-start | bytes 417800 | tf_op jit(solution)/shard_map/ppermute | solution.py:19
  360.2 4.5 collective-permute-start.9
  361.5 3.8 collective-permute-start.8
  365.4 12.9 %collective-permute-start.10 = (f32[2,68,256]{2,1,0:T(8,128)S(1)}, f32[2,68,256]{2,1,0:T(8,128)S(1)}, u32[]{:S(2)}, u32[]{:S(2)}) collective-permute-start(f32[2,68,256]{2,1,0:T(8,128)S(1)} %get-tuple-element.162), channel_id=1, source_target_pairs={{1,0},{2,1},{3,2},{4,3},{5,4},{6,5},{7,6},{8,7},{9,8},{10,9},{11,1... | collective-permute-start | bytes 417800 | tf_op jit(solution)/shard_map/ppermute | solution.py:21
  366.7 11.6 %collective-permute-start.11 = (f32[2,68,256]{2,1,0:T(8,128)S(1)}, f32[2,68,256]{2,1,0:T(8,128)S(1)}, u32[]{:S(2)}, u32[]{:S(2)}) collective-permute-start(f32[2,68,256]{2,1,0:T(8,128)S(1)} %get-tuple-element.163), channel_id=1, source_target_pairs={{0,1},{1,2},{2,3},{3,4},{4,5},{5,6},{6,7},{7,8},{8,9},{9,10},{10,1... | collective-permute-start | bytes 417800 | tf_op jit(solution)/shard_map/ppermute | solution.py:19
  531.7 4.5 collective-permute-start.13
  533.0 3.8 collective-permute-start.12
  536.9 9.6 %collective-permute-start.15 = (f32[2,68,256]{2,1,0:T(8,128)S(1)}, f32[2,68,256]{2,1,0:T(8,128)S(1)}, u32[]{:S(2)}, u32[]{:S(2)}) collective-permute-start(f32[2,68,256]{2,1,0:T(8,128)S(1)} %get-tuple-element.161), channel_id=1, source_target_pairs={{0,1},{1,2},{2,3},{3,4},{4,5},{5,6},{6,7},{7,8},{8,9},{9,10},{10,1... | collective-permute-start | bytes 417800 | tf_op jit(solution)/shard_map/ppermute | solution.py:19
  543.0 7.7 %collective-permute-start.14 = (f32[2,68,256]{2,1,0:T(8,128)S(1)}, f32[2,68,256]{2,1,0:T(8,128)S(1)}, u32[]{:S(2)}, u32[]{:S(2)}) collective-permute-start(f32[2,68,256]{2,1,0:T(8,128)S(1)} %get-tuple-element.160), channel_id=1, source_target_pairs={{1,0},{2,1},{3,2},{4,3},{5,4},{6,5},{7,6},{8,7},{9,8},{10,9},{11,1... | collective-permute-start | bytes 417800 | tf_op jit(solution)/shard_map/ppermute | solution.py:21
where the time goes:
time: 720 us; the launch traced here: 709 us
  blocking collectives  325 us (45%)
  matrix products  270 us (38%)
  starting transfers between devices  41.6 us (6%)
  other arithmetic  33.5 us (5%)
  waiting for transfers between devices  16.6 us (2%)
  local copies, waits for them, and re-layouts  13.3 us (2%)
  between operations  9.55 us (1%)
    psum x4, blocking collectives, body(): lax.psum(project(basis_vectors, created, image), ('gy', 'gx')) / cell_count  167 us
    psum x4, blocking collectives, body(): lax.psum((project(basis_vectors, created, first_rest), jnp.sum(first_rest...  158 us
    dot_general x8, matrix products, project(): jnp.einsum('kxyz,xyz->k', basis_vectors, image, precision=lax.Precision.H...  126 us
    dot_general x8, matrix products, combine(): jnp.einsum('k,kxyz->xyz', weights[:keep_count], basis_vectors, precision=...  116 us
    ppermute x8, starting transfers between devices, with_halo(): lax.ppermute(tail, axis, [(i, (i + 1) % count) for i in range(ends)])  30.8 us
    dot_general x1, matrix products, body(): jnp.einsum('axyz,bxyz->ab', basis_vectors, basis_vectors, precision=lax.P...  25.4 us
  transfers between devices with their start and end apart: 16, of which 8 were waited for; matrix products, arithmetic and copies ran while one was open for 6% of the time, Pallas kernels for 0%

commit v1 on v0

--- a/solution.py
+++ b/solution.py
@@ -92,7 +92,13 @@
         current = keep_count + section
         vector_now = basis_vectors[keep_count - 1] if section == 0 else created[-1]
         image = apply_operator(vector_now, reaction)
-        first_terms = lax.psum(project(basis_vectors, created, image), ("gy", "gx")) / cell_count
+
+        def _open_islands(buf, across):
+            return lax.all_gather(buf, axis_name=across).sum(axis=0)
+
+        first_terms = (
+            _open_islands(project(basis_vectors, created, image), ("gy", "gx")) / cell_count
+        )
         first_rest = image - combine(basis_vectors, created, first_terms)
         second_terms, rest_square = lax.psum(
             (project(basis_vectors, created, first_rest), jnp.sum(first_rest * first_rest)),

time: 720 us -> 724 us (level)
    unnamed x0 -> x4, blocking collectives: none -> 168 us
    psum x4 -> x0, blocking collectives: 167 us -> none  [body(): lax.psum(project(basis_vectors, created, image), ('gy', 'gx')) / cell_count]
where the time goes in v1:
time: 724 us; the launch traced here: 713 us
  blocking collectives  326 us (45%)
  matrix products  272 us (38%)
  starting transfers between devices  41.4 us (6%)
  other arithmetic  33.9 us (5%)
  waiting for transfers between devices  16.5 us (2%)
  local copies, waits for them, and re-layouts  13.8 us (2%)
  between operations  9.51 us (1%)
    unnamed x4, blocking collectives  168 us
    psum x4, blocking collectives, body(): lax.psum((project(basis_vectors, created, first_rest), jnp.sum(first_rest...  158 us
    dot_general x8, matrix products, project(): jnp.einsum('kxyz,xyz->k', basis_vectors, image, precision=lax.Precision.H...  128 us
    dot_general x8, matrix products, combine(): jnp.einsum('k,kxyz->xyz', weights[:keep_count], basis_vectors, precision=...  116 us
    ppermute x8, starting transfers between devices, with_halo(): lax.ppermute(tail, axis, [(i, (i + 1) % count) for i in range(ends)])  30.8 us
    dot_general x1, matrix products, body(): jnp.einsum('axyz,bxyz->ab', basis_vectors, basis_vectors, precision=lax.P...  25.4 us
  transfers between devices with their start and end apart: 16, of which 8 were waited for; matrix products, arithmetic and copies ran while one was open for 6% of the time, Pallas kernels for 0%

profile of v1, /device:TPU:0, one launch (start us, length us, event | category | flops | bytes accessed | tf_op | source)
XLA Modules:
  0.0 713.0 jit_solution(128027798658046270)
XLA Ops:
  1.7 1.3 collective-permute-start.1
  3.0 3.0 collective-permute-start
  6.1 25.4 %fusion.34 = f32[36,36]{1,0:T(8,128)S(1)} fusion(f32[36,4,64,256]{3,2,1,0:T(8,128)} %param.22), kind=kOutput, calls=%fused_computation.34 | convolution fusion | flops 1019215872 | bytes 9442368 | tf_op jit(solution)/shard_map/axyz,bxyz->ab/dot_general | solution.py:84
  34.8 4.9 collective-permute-start.3
  39.7 1.6 collective-permute-start.2
  42.3 5.0 collective-permute-done.2
  47.8 15.8 %fusion.38 = f32[36]{0:T(128)S(1)} fusion(f32[36,4,64,256]{3,2,1,0:T(8,128)} %param.22, f32[4,64,256,1]{2,1,0,3:T(8,128)S(1)} %bitcast.235), kind=kOutput, calls=%fused_computation.40 | convolution fusion | flops 28311552 | bytes 9699472 | tf_op jit(solution)/shard_map/kxyz,xyz->k/dot_general | solution.py:57
  63.9 42.2 %all-reduce.5 = f32[1152]{0:T(1024)S(1)} all-reduce(f32[1152]{0:T(1024)S(1)} %dynamic-update-slice.20), channel_id=2, replica_groups=mesh['gy'=2,'gx'=16] {'gy','gx'}, use_global_device_ids=true, to_apply=%add.5 | all-reduce | flops 1152 | bytes 9216
  106.2 14.5 %fusion.26 = f32[1,4,64,256]{3,0,2,1:T(1,128)S(1)} fusion(f32[36,4,64,256]{3,2,1,0:T(8,128)} %param.22, f32[36]{0:T(128)S(1)} %reduce_sum.252), kind=kOutput, calls=%fused_computation.26 | convolution fusion | flops 28311588 | bytes 9699472 | tf_op jit(solution)/shard_map/k,kxyz->xyz/dot_general | solution.py:64
  121.3 16.0 %fusion.41 = f32[36]{0:T(128)S(1)} fusion(f32[36,4,64,256]{3,2,1,0:T(8,128)} %param.22, f32[4,64,256,1]{2,1,0,3:T(8,128)S(1)} %get-tuple-element.159), kind=kOutput, calls=%fused_computation.41 | convolution fusion | flops 28311552 | bytes 9699472 | tf_op jit(solution)/shard_map/kxyz,xyz->k/dot_general | solution.py:57
  137.3 39.7 %all-reduce.12 = (f32[36]{0:T(128)S(1)}, f32[]{:T(128)}, f32[36,36]{1,0:T(8,128)S(1)}) all-reduce(f32[36]{0:T(128)S(1)} %fusion.41, f32[]{:T(128)} %get-tuple-element.158, f32[36,36]{1,0:T(8,128)S(1)} %fusion.34), channel_id=1, replica_groups=mesh['gy'=2,'gx'=16] {'gy','gx'}, use_global_device_ids=true, to_apply=%region_1.0 | all-reduce | flops 1333 | bytes 10664 | tf_op jit(solution)/shard_map/psum | solution.py:103
  177.8 14.5 %fusion.22 = f32[1,4,64,256]{3,0,2,1:T(1,128)S(1)} fusion(f32[36,4,64,256]{3,2,1,0:T(8,128)} %param.22, f32[36]{0:T(128)S(1)} %get-tuple-element.148), kind=kOutput, calls=%fused_computation.22 | convolution fusion | flops 28311588 | bytes 9699472 | tf_op jit(solution)/shard_map/k,kxyz->xyz/dot_general | solution.py:64
  194.4 1.3 collective-permute-start.5
  195.7 3.0 collective-permute-start.4
  199.6 1.3 collective-permute-start.6
  200.9 4.8 collective-permute-start.7
  205.8 1.9 dynamic-slice_select_fusion.2
  207.7 1.7 scatter.35
  209.7 2.1 collective-permute-done.7
  211.9 1.0 multiply_reduce_fusion.14
  213.0 16.1 %fusion.44 = f32[36]{0:T(128)S(1)} fusion(f32[36,4,64,256]{3,2,1,0:T(8,128)} %param.22, f32[4,64,256,1]{2,1,0,3:T(8,128)S(1)} %bitcast.241), kind=kOutput, calls=%fused_computation.42 | convolution fusion | flops 28311552 | bytes 9699472 | tf_op jit(solution)/shard_map/kxyz,xyz->k/dot_general | solution.py:57
  229.9 41.9 %all-reduce.6 = f32[1184]{0:T(1024)S(1)} all-reduce(f32[1184]{0:T(1024)S(1)} %maximum_dynamic-update-slice_fusion), channel_id=3, replica_groups=mesh['gy'=2,'gx'=16] {'gy','gx'}, use_global_device_ids=true, to_apply=%add.6 | all-reduce | flops 1184 | bytes 9472
  272.5 14.5 %fusion.18 = f32[1,4,64,256]{3,0,2,1:T(1,128)S(1)} fusion(f32[36,4,64,256]{3,2,1,0:T(8,128)} %param.22, f32[37]{0:T(128)S(1)} %broadcast_multiply_fusion.6), kind=kOutput, calls=%fused_computation.18 | convolution fusion | flops 28311552 | bytes 9699476 | tf_op jit(solution)/shard_map/k,kxyz->xyz/dot_general | solution.py:64
  287.0 1.4 multiply_reduce_fusion.12
  288.4 16.0 %fusion.47 = f32[36]{0:T(128)S(1)} fusion(f32[36,4,64,256]{3,2,1,0:T(8,128)} %param.22, f32[4,64,256,1]{2,1,0,3:T(8,128)S(1)} %bitcast.236), kind=kOutput, calls=%fused_computation.43 | convolution fusion | flops 28311552 | bytes 9699472 | tf_op jit(solution)/shard_map/kxyz,xyz->k/dot_general | solution.py:57
  305.2 39.8 %all-reduce.11 = (f32[37]{0:T(128)S(1)}, f32[]{:T(128)}) all-reduce(f32[37]{0:T(128)S(1)} %pad_maximum_fusion.26, f32[]{:T(128)} %get-tuple-element.134), channel_id=1, replica_groups=mesh['gy'=2,'gx'=16] {'gy','gx'}, use_global_device_ids=true, to_apply=%region_10.11 | all-reduce | flops 38 | bytes 304 | tf_op jit(solution)/shard_map/psum | solution.py:103
  348.3 14.5 %fusion.14 = f32[1,4,64,256]{3,0,2,1:T(1,128)S(1)} fusion(f32[36,4,64,256]{3,2,1,0:T(8,128)} %param.22, f32[37]{0:T(128)S(1)} %get-tuple-element.197), kind=kOutput, calls=%fused_computation.14 | convolution fusion | flops 28311552 | bytes 9699476 | tf_op jit(solution)/shard_map/k,kxyz->xyz/dot_general | solution.py:64
  363.4 1.3 collective-permute-start.9
  364.7 3.0 collective-permute-start.8
  368.6 1.3 collective-permute-start.10
  369.9 4.8 collective-permute-start.11
  374.7 1.9 dynamic-slice_select_fusion.1
  376.7 1.7 scatter.40
  378.8 2.7 collective-permute-done.11
  381.5 1.1 multiply_reduce_fusion.11
  382.7 16.1 %fusion.50 = f32[36]{0:T(128)S(1)} fusion(f32[36,4,64,256]{3,2,1,0:T(8,128)} %param.22, f32[4,64,256,1]{2,1,0,3:T(8,128)S(1)} %bitcast.240), kind=kOutput, calls=%fused_computation.44 | convolution fusion | flops 28311552 | bytes 9699472 | tf_op jit(solution)/shard_map/kxyz,xyz->k/dot_general | solution.py:57
  398.7 1.5 maximum_dynamic-update-slice_fusion.1
  400.2 42.1 %all-reduce.7 = f32[1216]{0:T(1024)S(1)} all-reduce(f32[1216]{0:T(1024)S(1)} %maximum_dynamic-update-slice_fusion.1), channel_id=4, replica_groups=mesh['gy'=2,'gx'=16] {'gy','gx'}, use_global_device_ids=true, to_apply=%add.7 | all-reduce | flops 1216 | bytes 9728
  443.1 14.5 %fusion.10 = f32[1,4,64,256]{3,0,2,1:T(1,128)S(1)} fusion(f32[36,4,64,256]{3,2,1,0:T(8,128)} %param.22, f32[38]{0:T(128)S(1)} %broadcast_multiply_fusion.4), kind=kOutput, calls=%fused_computation.10 | convolution fusion | flops 28311552 | bytes 9699480 | tf_op jit(solution)/shard_map/k,kxyz->xyz/dot_general | solution.py:64
  457.5 2.0 multiply_reduce_fusion.7
  459.5 16.0 %fusion.53 = f32[36]{0:T(128)S(1)} fusion(f32[36,4,64,256]{3,2,1,0:T(8,128)} %param.22, f32[4,64,256,1]{2,1,0,3:T(8,128)S(1)} %bitcast.239), kind=kOutput, calls=%fused_computation.45 | convolution fusion | flops 28311552 | bytes 9699472 | tf_op jit(solution)/shard_map/kxyz,xyz->k/dot_general | solution.py:57
  475.5 1.3 pad_maximum_fusion.27
  476.8 39.0 %all-reduce.10 = (f32[38]{0:T(128)S(1)}, f32[]{:T(128)}) all-reduce(f32[38]{0:T(128)S(1)} %pad_maximum_fusion.27, f32[]{:T(128)} %get-tuple-element.129), channel_id=1, replica_groups=mesh['gy'=2,'gx'=16] {'gy','gx'}, use_global_device_ids=true, to_apply=%region_21.22 | all-reduce | flops 39 | bytes 312 | tf_op jit(solution)/shard_map/psum | solution.py:103
  519.3 14.5 %fusion.6 = f32[1,4,64,256]{3,0,2,1:T(1,128)S(1)} fusion(f32[36,4,64,256]{3,2,1,0:T(8,128)} %param.22, f32[38]{0:T(128)S(1)} %get-tuple-element.188), kind=kOutput, calls=%fused_computation.6 | convolution fusion | flops 28311552 | bytes 9699480 | tf_op jit(solution)/shard_map/k,kxyz->xyz/dot_general | solution.py:64
  533.8 1.3 fusion.141
  535.1 1.3 collective-permute-start.13
  536.4 3.0 collective-permute-start.12
  540.3 4.2 collective-permute-start.15
  544.5 2.0 dynamic-slice_select_fusion
  546.5 1.3 collective-permute-start.14
  547.9 1.6 scatter.45
  549.9 4.2 collective-permute-done.14
  554.2 1.1 multiply_reduce_fusion.6
  555.3 16.1 %fusion.56 = f32[36]{0:T(128)S(1)} fusion(f32[36,4,64,256]{3,2,1,0:T(8,128)} %param.22, f32[4,64,256,1]{2,1,0,3:T(8,128)S(1)} %bitcast.237), kind=kOutput, calls=%fused_computation.46 | convolution fusion | flops 28311552 | bytes 9699472 | tf_op jit(solution)/shard_map/kxyz,xyz->k/dot_general | solution.py:57
  571.4 2.2 maximum_dynamic-update-slice_fusion.2
  573.6 41.8 %all-reduce.8 = f32[1248]{0:T(1024)S(1)} all-reduce(f32[1248]{0:T(1024)S(1)} %maximum_dynamic-update-slice_fusion.2), channel_id=5, replica_groups=mesh['gy'=2,'gx'=16] {'gy','gx'}, use_global_device_ids=true, to_apply=%add.8 | all-reduce | flops 1248 | bytes 9984
  616.2 14.5 %fusion.2 = f32[1,4,64,256]{3,0,2,1:T(1,128)S(1)} fusion(f32[36,4,64,256]{3,2,1,0:T(8,128)} %param.22, f32[39]{0:T(128)S(1)} %broadcast_multiply_fusion.2), kind=kOutput, calls=%fused_computation.2 | convolution fusion | flops 28311552 | bytes 9699484 | tf_op jit(solution)/shard_map/k,kxyz->xyz/dot_general | solution.py:64
  630.6 2.8 multiply_reduce_fusion
  633.5 16.0 %fusion.59 = f32[36]{0:T(128)S(1)} fusion(f32[36,4,64,256]{3,2,1,0:T(8,128)} %param.22, f32[4,64,256,1]{2,1,0,3:T(8,128)S(1)} %bitcast.238), kind=kOutput, calls=%fused_computation.47 | convolution fusion | flops 28311552 | bytes 9699472 | tf_op jit(solution)/shard_map/kxyz,xyz->k/dot_general | solution.py:57
  649.4 2.0 pad_maximum_fusion.28
  651.4 39.2 %all-reduce.9 = (f32[39]{0:T(128)S(1)}, f32[]{:T(128)}) all-reduce(f32[39]{0:T(128)S(1)} %pad_maximum_fusion.28, f32[]{:T(128)} %get-tuple-element.122), channel_id=1, replica_groups=mesh['gy'=2,'gx'=16] {'gy','gx'}, use_global_device_ids=true, to_apply=%region_34.35 | all-reduce | flops 40 | bytes 320 | tf_op jit(solution)/shard_map/psum | solution.py:103
  691.9 14.5 %fusion.28 = f32[1,4,64,256]{3,0,2,1:T(1,128)S(1)} fusion(f32[36,4,64,256]{3,2,1,0:T(8,128)} %param.22, f32[39]{0:T(128)S(1)} %get-tuple-element.181), kind=kOutput, calls=%fused_computation.28 | convolution fusion | flops 28311552 | bytes 9699484 | tf_op jit(solution)/shard_map/k,kxyz->xyz/dot_general | solution.py:64
  709.8 2.0 fusion.135
  711.7 1.1 pad_maximum_fusion
  (100 shorter events, 21.6 us)
Async XLA Ops:
  0.6 30.8 %copy-start.1 = (s32[2]{0:T(128)S(1)}, s32[2]{0:T(128)}, u32[]{:S(2)}) copy-start(s32[2]{0:T(128)} %constant.309.clone.1) | copy-start | bytes 28
  0.6 31.5 %copy-start.3 = (s32[2]{0:T(128)S(1)}, s32[2]{0:T(128)}, u32[]{:S(2)}) copy-start(s32[2]{0:T(128)} %constant.307.clone.1) | copy-start | bytes 28
  0.7 32.2 %copy-start.2 = (s32[2]{0:T(128)S(1)}, s32[2]{0:T(128)}, u32[]{:S(2)}) copy-start(s32[2]{0:T(128)} %constant.304.clone.1) | copy-start | bytes 28
  0.7 46.7 %copy-start = (f32[4,64,256]{2,1,0:T(8,128)S(1)}, f32[4,64,256]{2,1,0:T(8,128)}, u32[]{:S(2)}) copy-start(f32[4,64,256]{2,1,0:T(8,128)} %param.23) | copy-start | bytes 786436
  1.7 33.0 %collective-permute-start.1 = (f32[4,2,256]{2,1,0:T(2,128)S(1)}, f32[4,2,256]{2,1,0:T(2,128)S(1)}, u32[]{:S(2)}, u32[]{:S(2)}) collective-permute-start(f32[4,2,256]{2,1,0:T(2,128)S(1)} %get-tuple-element.174), channel_id=1, source_target_pairs={{16,0},{17,1},{18,2},{19,3},{20,4},{21,5},{22,6},{23,7},{24,8},{25... | collective-permute-start | bytes 24584 | tf_op jit(solution)/shard_map/ppermute | solution.py:21
  3.0 31.7 %collective-permute-start = (f32[4,2,256]{2,1,0:T(2,128)S(1)}, f32[4,2,256]{2,1,0:T(2,128)S(1)}, u32[]{:S(2)}, u32[]{:S(2)}) collective-permute-start(f32[4,2,256]{2,1,0:T(2,128)S(1)} %get-tuple-element.175), channel_id=1, source_target_pairs={{0,16},{1,17},{2,18},{3,19},{4,20},{5,21},{6,22},{7,23},{8,24},{9,... | collective-permute-start | bytes 24584 | tf_op jit(solution)/shard_map/ppermute | solution.py:19
  34.8 7.5 %collective-permute-start.3 = (f32[2,68,256]{2,1,0:T(8,128)S(1)}, f32[2,68,256]{2,1,0:T(8,128)S(1)}, u32[]{:S(2)}, u32[]{:S(2)}) collective-permute-start(f32[2,68,256]{2,1,0:T(8,128)S(1)} %get-tuple-element.167), channel_id=1, source_target_pairs={{0,1},{1,2},{2,3},{3,4},{4,5},{5,6},{6,7},{7,8},{8,9},{9,10},{10,1... | collective-permute-start | bytes 417800 | tf_op jit(solution)/shard_map/ppermute | solution.py:19
  39.7 7.7 %collective-permute-start.2 = (f32[2,68,256]{2,1,0:T(8,128)S(1)}, f32[2,68,256]{2,1,0:T(8,128)S(1)}, u32[]{:S(2)}, u32[]{:S(2)}) collective-permute-start(f32[2,68,256]{2,1,0:T(8,128)S(1)} %get-tuple-element.166), channel_id=1, source_target_pairs={{1,0},{2,1},{3,2},{4,3},{5,4},{6,5},{7,6},{8,7},{9,8},{10,9},{11,1... | collective-permute-start | bytes 417800 | tf_op jit(solution)/shard_map/ppermute | solution.py:21
  194.4 4.5 collective-permute-start.5
  195.7 3.8 collective-permute-start.4
  199.6 12.3 %collective-permute-start.6 = (f32[2,68,256]{2,1,0:T(8,128)S(1)}, f32[2,68,256]{2,1,0:T(8,128)S(1)}, u32[]{:S(2)}, u32[]{:S(2)}) collective-permute-start(f32[2,68,256]{2,1,0:T(8,128)S(1)} %get-tuple-element.164), channel_id=1, source_target_pairs={{1,0},{2,1},{3,2},{4,3},{5,4},{6,5},{7,6},{8,7},{9,8},{10,9},{11,1... | collective-permute-start | bytes 417800 | tf_op jit(solution)/shard_map/ppermute | solution.py:21
  200.9 10.9 %collective-permute-start.7 = (f32[2,68,256]{2,1,0:T(8,128)S(1)}, f32[2,68,256]{2,1,0:T(8,128)S(1)}, u32[]{:S(2)}, u32[]{:S(2)}) collective-permute-start(f32[2,68,256]{2,1,0:T(8,128)S(1)} %get-tuple-element.165), channel_id=1, source_target_pairs={{0,1},{1,2},{2,3},{3,4},{4,5},{5,6},{6,7},{7,8},{8,9},{9,10},{10,1... | collective-permute-start | bytes 417800 | tf_op jit(solution)/shard_map/ppermute | solution.py:19
  363.4 4.5 collective-permute-start.9
  364.7 3.8 collective-permute-start.8
  368.6 12.9 %collective-permute-start.10 = (f32[2,68,256]{2,1,0:T(8,128)S(1)}, f32[2,68,256]{2,1,0:T(8,128)S(1)}, u32[]{:S(2)}, u32[]{:S(2)}) collective-permute-start(f32[2,68,256]{2,1,0:T(8,128)S(1)} %get-tuple-element.162), channel_id=1, source_target_pairs={{1,0},{2,1},{3,2},{4,3},{5,4},{6,5},{7,6},{8,7},{9,8},{10,9},{11,1... | collective-permute-start | bytes 417800 | tf_op jit(solution)/shard_map/ppermute | solution.py:21
  369.9 11.6 %collective-permute-start.11 = (f32[2,68,256]{2,1,0:T(8,128)S(1)}, f32[2,68,256]{2,1,0:T(8,128)S(1)}, u32[]{:S(2)}, u32[]{:S(2)}) collective-permute-start(f32[2,68,256]{2,1,0:T(8,128)S(1)} %get-tuple-element.163), channel_id=1, source_target_pairs={{0,1},{1,2},{2,3},{3,4},{4,5},{5,6},{6,7},{7,8},{8,9},{9,10},{10,1... | collective-permute-start | bytes 417800 | tf_op jit(solution)/shard_map/ppermute | solution.py:19
  535.1 4.5 collective-permute-start.13
  536.4 3.8 collective-permute-start.12
  540.3 9.6 %collective-permute-start.15 = (f32[2,68,256]{2,1,0:T(8,128)S(1)}, f32[2,68,256]{2,1,0:T(8,128)S(1)}, u32[]{:S(2)}, u32[]{:S(2)}) collective-permute-start(f32[2,68,256]{2,1,0:T(8,128)S(1)} %get-tuple-element.161), channel_id=1, source_target_pairs={{0,1},{1,2},{2,3},{3,4},{4,5},{5,6},{6,7},{7,8},{8,9},{9,10},{10,1... | collective-permute-start | bytes 417800 | tf_op jit(solution)/shard_map/ppermute | solution.py:19
  546.5 7.7 %collective-permute-start.14 = (f32[2,68,256]{2,1,0:T(8,128)S(1)}, f32[2,68,256]{2,1,0:T(8,128)S(1)}, u32[]{:S(2)}, u32[]{:S(2)}) collective-permute-start(f32[2,68,256]{2,1,0:T(8,128)S(1)} %get-tuple-element.160), channel_id=1, source_target_pairs={{1,0},{2,1},{3,2},{4,3},{5,4},{6,5},{7,6},{8,7},{9,8},{10,9},{11,1... | collective-permute-start | bytes 417800 | tf_op jit(solution)/shard_map/ppermute | solution.py:21
